TPU v7x, 128 devices: a whole 4x4x4 slice. The times are simulated.
128 devices in a mesh: dp: 8 (over y, core), tensor: 16 (over x, z).
Axes of the slice: x: 4, y: 4, z: 4, core: 2. Of those that a mesh axis runs over, the one named last changes fastest.
Arguments:
- inputs: bfloat16 [24576, 5120], P('dp', 'tensor'), may hold values from -6 to 6
- cotangent: bfloat16 [24576, 4096], P('dp', 'tensor'), may hold values from -192 to 192
- lengths: int32 [64], P('dp'), may hold values from 96 to 384
- momentum: float32 [8, 4096, 5120], P('dp', 'tensor'), may hold values from -26 to 26
- weight: bfloat16 [4096, 5120], P('tensor'), may hold values from -0.00039863586 to 0.00039863586
- right_factor: float32 [5120, 64], replicated, may hold values from -1 to 1
Outputs:
- new_weight: bfloat16 [4096, 5120], P('tensor')
- new_momentum: float32 [8, 4096, 5120], P('dp', 'tensor')
- new_right: float32 [5120, 64], replicated
Inputs may be any that keep to these rules, and one draw needn't show every extreme that they name: The first lengths[i] positions of block i are real tokens, the rest padding.
All inputs are finite; a program needn't handle non-finite values.
Results may differ from a plain program's by a relative error of at most 0.00045.
Values may be sent and summed in bfloat16 or wider, within the bound.
A program may use at most 128 MiB of HBM per device.

v0:
```python
import math
import jax
import jax.numpy as jnp
from jax import lax
from jax.sharding import PartitionSpec as P

EPS = 1e-06
MU = 0.95
LR = 0.02


def from_everyone(x, axis):
    devices = lax.axis_size(axis)
    return lax.all_to_all(jnp.broadcast_to(x[None], (devices, *x.shape)), axis, 0, 0, tiled=True)


def over_copies(x, axis):
    return from_everyone(x, axis).sum(axis=0)


def per_device(inputs, cotangent, lengths, momentum, weight, right_factor):
    hi = lax.Precision.HIGHEST
    contract = (((0,), (0,)), ((), ()))
    replicas = lax.axis_size("dp")
    block_len = inputs.shape[0] // lengths.shape[0]
    position = jnp.arange(block_len, dtype=jnp.int32)
    keep = (position[None, :] < lengths[:, None]).reshape(-1).astype(jnp.bfloat16)
    masked = inputs * keep[:, None]
    count = jnp.sum(lengths.astype(jnp.float32))
    grad = lax.dot_general(
        cotangent,
        lax.all_gather(masked, "tensor", axis=1, tiled=True),
        contract,
        preferred_element_type=jnp.float32,
    )
    both = momentum[0] + grad / count
    left = over_copies(jnp.dot(both, right_factor, precision=hi), "dp") / replicas
    gram = over_copies(jnp.dot(left.T, left, precision=hi), "tensor")
    factor = jnp.linalg.cholesky(gram)
    ortho = jax.scipy.linalg.solve_triangular(factor, left.T, lower=True).T
    term = lax.dot_general(both, ortho, contract, precision=hi) / replicas
    right = lax.psum(term, ("dp", "tensor"))
    squares = jnp.sum(right * right, axis=0)
    new_right = right * lax.rsqrt(squares + EPS)
    lowrank = jnp.dot(ortho, right.T, precision=hi)
    new_momentum = (both - (1.0 - MU) * lowrank)[None]
    rows_all = ortho.shape[0] * lax.axis_size("tensor")
    update = jnp.dot(ortho, new_right.T, precision=hi)
    new_weight = (
        weight.astype(jnp.float32) - LR * math.sqrt(rows_all / right.shape[0]) * update
    ).astype(jnp.bfloat16)
    return (new_weight, new_momentum, new_right)


def solution(mesh):
    placed = (
        P("dp", "tensor"),
        P("dp", "tensor"),
        P("dp"),
        P("dp", "tensor", None),
        P("tensor", None),
        P(),
    )
    return jax.shard_map(
        per_device,
        mesh=mesh,
        in_specs=placed,
        out_specs=(P("tensor", None), P("dp", "tensor", None), P()),
        check_vma=False,
    )
```

profile of v0, /device:TPU:1, one launch (start us, length us, event | category | flops | bytes accessed | tf_op | source)
XLA Modules:
  0.0 449.7 jit_solution(14454124653131563446)
XLA Ops:
  7.2 0.8 fusion.15
  8.1 3.0 broadcast_multiply_fusion
  11.1 5.9 %copy.22 = f32[1,256,5120]{1,2,0:T(8,128)} copy(f32[1,256,5120]{2,1,0:T(8,128)} %param.9) | data formatting | bytes 10485760 | tf_op args[3]
  17.0 0.6 convert_reduce_fusion
  17.6 183.0 %all-gather.2.cloned.1.call-done = bf16[3072,5120]{0,1:T(8,128)(2,1)} async-done(((bf16[3072,320]{0,1:T(8,128)(2,1)}), bf16[3072,5120]{0,1:T(8,128)(2,1)}) %all-gather.2.cloned.1.call-update) | async-done | bytes 31457296 | tf_op jit(solution)/shard_map/all_gather | solution.py:32
  200.6 17.1 %fusion.5 = f32[256,5120]{0,1:T(8,128)S(1)} fusion(bf16[3072,5120]{0,1:T(8,128)(2,1)} %all-gather.2.cloned.1.call-done, bf16[3072,256]{1,0:T(8,128)(2,1)S(1)} %copy-done, f32[1,256,5120]{1,2,0:T(8,128)} %copy.22, f32[]{:T(128)} %convert_reduce_fusion), kind=kOutput, calls=%fused_computation.8 | convolution fusion | flops 8055685120 | bytes 43515908 | tf_op jit(solution)/shard_map/dot_general | solution.py:30
  217.7 3.2 fusion.18
  221.0 14.2 %all_to_all.10 = f32[8,256,64]{1,2,0:T(8,128)S(1)} all-to-all(f32[8,256,64]{1,2,0:T(8,128)S(1)} %broadcast_in_dim.7), channel_id=1, replica_groups=mesh['dp'=8,'tensor'=16] {'dp'}, dimensions={0} | all-to-all | bytes 1048576 | tf_op jit(solution)/shard_map/all_to_all | solution.py:14
  235.5 0.3 reshape.40
  235.8 12.2 %all_to_all.11 = f32[16,1,4096]{2,1,0:T(1,128)S(1)} all-to-all(f32[16,1,4096]{2,1,0:T(1,128)S(1)} %reshape.40), channel_id=1, replica_groups=mesh['dp'=8,'tensor'=16] {'tensor'}, dimensions={0} | all-to-all | bytes 524288 | tf_op jit(solution)/shard_map/all_to_all | solution.py:14
  248.1 0.5 broadcast.66
  248.6 1.3 reduce.6
  250.2 5.8 %cholesky.16 = f32[64,64]{1,0:T(8,128)S(1)} custom-call(f32[64,64]{1,0:T(8,128)S(1)} %fusion.12), custom_call_target="Cholesky" | custom-call | tf_op jit(solution)/shard_map/jit(cholesky)/cholesky | solution.py:39
  256.1 0.6 compare_reduce_fusion
  256.7 0.7 fusion.10
  257.4 4.9 %custom-call.7 = f32[1,64,64]{1,2,0:T(8,128)S(1)} custom-call(f32[1,64,64]{2,1,0:T(8,128)S(1)} %fusion.10), custom_call_target="InvertDiagBlocksLowerTriangular" | custom-call | tf_op jit(solution)/shard_map/jit(_solve_triangular)/triangular_solve | solution.py:40
  262.3 0.3 fusion.6
  262.6 8.7 %convolution_multiply_fusion.2 = f32[5120,64]{0,1:T(8,128)} fusion(f32[256,5120]{0,1:T(8,128)} %copy-done.2, f32[64,256]{1,0:T(8,128)S(1)} %fusion.6), kind=kOutput, calls=%fused_computation.9 | convolution fusion | flops 1006960640 | bytes 6619136 | tf_op jit(solution)/shard_map/dot_general | solution.py:41
  271.3 146.8 %all-reduce.2.cloned.1.call-done = f32[5120,64]{0,1:T(8,128)} async-done(((f32[5120,64]{0,1:T(8,128)}), f32[5120,64]{0,1:T(8,128)}) %all-reduce.2.cloned.1.call-update) | async-done | bytes 1310736 | tf_op jit(solution)/shard_map/psum | solution.py:42
  418.1 1.5 multiply_reduce_fusion
  419.6 9.7 %fusion.2 = f32[1,256,5120]{1,2,0:T(8,128)} fusion(f32[256,5120]{0,1:T(8,128)} %copy-done.2, f32[64,256]{1,0:T(8,128)S(1)} %fusion.6, f32[5120,64]{0,1:T(8,128)} %all-reduce.2.cloned.1.call-done), kind=kOutput, calls=%fused_computation.4 | convolution fusion | flops 1009254400 | bytes 11862016 | tf_op jit(solution)/shard_map/dot_general | solution.py:45
  429.3 6.0 %copy.25 = f32[1,256,5120]{2,1,0:T(8,128)} copy(f32[1,256,5120]{1,2,0:T(8,128)} %fusion.2) | data formatting | bytes 10485760
  435.5 1.6 copy-done.5
  437.1 5.8 %fusion.3 = bf16[256,5120]{1,0:T(8,128)(2,1)} fusion(f32[64,256]{1,0:T(8,128)S(1)} %fusion.6, f32[5120,64]{0,1:T(8,128)S(1)} %broadcast_multiply_fusion.1, bf16[256,5120]{1,0:T(8,128)(2,1)S(1)} %copy-done.5), kind=kOutput, calls=%fused_computation.5 | convolution fusion | flops 1011875840 | bytes 6619136 | tf_op jit(solution)/shard_map/dot_general | solution.py:48
  (31 shorter events, 1.0 us)
Async XLA Ops:
  7.2 193.5 %copy-start = (bf16[3072,256]{1,0:T(8,128)(2,1)S(1)}, bf16[3072,256]{1,0:T(8,128)(2,1)}, u32[]{:S(2)}) copy-start(bf16[3072,256]{1,0:T(8,128)(2,1)} %param.7) | copy-start | bytes 4718596
  7.2 193.5 %all-gather.2.cloned.1.call-start = ((), (), s32[]{:S(2)}) async-start(), calls=%async_computation.2 | async-start | bytes 33423360 | tf_op jit(solution)/shard_map/all_gather | solution.py:32
  11.1 5.9 %copy-start.7 = (s32[8]{0:T(128)S(1)}, s32[8]{0:T(128)}, u32[]{:S(2)}) copy-start(s32[8]{0:T(128)} %param.8) | copy-start | bytes 100
  11.1 407.0 %all-reduce.2.cloned.1.call-start = ((), (), s32[]{:S(2)}) async-start(), calls=%async_computation.3 | async-start | bytes 2621440 | tf_op jit(solution)/shard_map/psum | solution.py:42
  17.6 200.1 %copy-start.6 = (f32[5120,64]{0,1:T(8,128)S(1)}, f32[5120,64]{0,1:T(8,128)}, u32[]{:S(2)}) copy-start(f32[5120,64]{0,1:T(8,128)} %param.11) | copy-start | bytes 3932164
  217.7 3.2 copy-start.2
  429.3 6.0 %copy-start.3 = (f32[5120,64]{0,1:T(8,128)S(1)}, f32[5120,64]{0,1:T(8,128)}, u32[]{:S(2)}) copy-start(f32[5120,64]{0,1:T(8,128)} %all-reduce.2.cloned.1.call-done) | copy-start | bytes 3932164
  435.3 1.7 copy-start.5
  435.3 7.6 %copy-start.1 = (bf16[3072,256]{1,0:T(8,128)(2,1)S(1)}, bf16[3072,256]{1,0:T(8,128)(2,1)}, u32[]{:S(2)}) copy-start(bf16[3072,256]{1,0:T(8,128)(2,1)} %param.7) | copy-start | bytes 4718596
  437.1 5.8 %copy-start.4 = (f32[5120,64]{0,1:T(8,128)}, f32[5120,64]{0,1:T(8,128)S(1)}, u32[]{:S(2)}) copy-start(f32[5120,64]{0,1:T(8,128)S(1)} %broadcast_multiply_fusion.1) | copy-start | bytes 3932164
Sparse Core Ops, SparseCore 0:
  11.2 189.4 all-gather.1
  271.4 146.6 all-reduce.1
where the time goes:
time: 450 us
  waiting for transfers between devices  330 us (73%)
  matrix products  44.9 us (10%)
  blocking collectives  26.5 us (6%)
  other arithmetic  19.5 us (4%)
  local copies, waits for them, and re-layouts  14.7 us (3%)
  between operations  14.2 us (3%)
    all_gather x1, waiting for transfers between devices, per_device(): lax.all_gather(masked, 'tensor', axis=1, tiled=True)  183 us
    psum x1, waiting for transfers between devices, per_device(): right = lax.psum(term, ('dp', 'tensor'))  147 us
    all_to_all x2, blocking collectives, from_everyone(): lax.all_to_all(jnp.broadcast_to(x[None], (devices, *x.shape)), axis, 0, 0...  26.5 us
    dot_general x1, matrix products, per_device(): lax.dot_general(cotangent, lax.all_gather(masked, 'tensor', axis=1, tiled...  17.1 us
    unnamed x20, local copies, waits for them, and re-layouts  14 us
    dot_general x1, matrix products, per_device(): lowrank = jnp.dot(ortho, right.T, precision=hi)  9.69 us
  transfers between devices with their start and end apart: 2, of which 2 were waited for; matrix products, arithmetic and copies ran while one was open for 1% of the time, Pallas kernels for 0%

commit v1 on v0

--- a/solution.py
+++ b/solution.py
@@ -29,7 +29,9 @@
     count = jnp.sum(lengths.astype(jnp.float32))
     grad = lax.dot_general(
         cotangent,
-        lax.all_gather(masked, "tensor", axis=1, tiled=True),
+        jnp.concatenate(
+            lax.all_to_all(jnp.stack([masked] * lax.axis_size("tensor")), "tensor", 0, 0), axis=1
+        ),
         contract,
         preferred_element_type=jnp.float32,
     )

time: 450 us -> 863 us (1.92)
  waiting for transfers between devices: 330 us -> 720 us
  local copies, waits for them, and re-layouts: 14.7 us -> 25.1 us
    all_to_all x0 -> x1, waiting for transfers between devices: none -> 573 us  [per_device(): lax.all_to_all(jnp.stack([masked] * lax.axis_size('tensor')), 'tensor', 0...]
    all_gather x1 -> x0, waiting for transfers between devices: 183 us -> none  [per_device(): lax.all_gather(masked, 'tensor', axis=1, tiled=True)]
    another operation x0 -> x1, local copies, waits for them, and re-layouts: none -> 10.6 us  [per_device(): jnp.stack([masked] * lax.axis_size('tensor'))]
where the time goes in v1:
time: 863 us; the launch traced here: 862 us
  waiting for transfers between devices  720 us (83%)
  matrix products  45 us (5%)
  blocking collectives  32.3 us (4%)
  local copies, waits for them, and re-layouts  25.1 us (3%)
  other arithmetic  16.9 us (2%)
  between operations  14.2 us (2%)
    all_to_all x1, waiting for transfers between devices, per_device(): lax.all_to_all(jnp.stack([masked] * lax.axis_size('tensor')), 'tensor', 0...  573 us
    psum x1, waiting for transfers between devices, per_device(): right = lax.psum(term, ('dp', 'tensor'))  147 us
    all_to_all x2, blocking collectives, from_everyone(): lax.all_to_all(jnp.broadcast_to(x[None], (devices, *x.shape)), axis, 0, 0...  32.3 us
  transfers between devices with their start and end apart: 2, of which 2 were waited for; matrix products, arithmetic and copies ran while one was open for 1% of the time, Pallas kernels for 0%

profile of v1, /device:TPU:1, one launch (start us, length us, event | category | flops | bytes accessed | tf_op | source)
XLA Modules:
  0.0 862.0 jit_solution(2959048698053935739)
XLA Ops:
  7.2 0.8 fusion.15
  8.0 1.7 broadcast_multiply_fusion
  9.7 10.6 %stack.2 = bf16[16,3072,320]{1,2,0:T(8,128)(2,1)} broadcast(bf16[3072,320]{0,1:T(8,128)(2,1)S(1)} %broadcast_multiply_fusion), dimensions={1,2} | broadcast | bytes 33423360 | tf_op jit(solution)/shard_map/stack | solution.py:33
  20.4 8.5 all-to-all-start
  28.9 5.9 copy.28
  34.8 0.6 convert_reduce_fusion
  35.4 573.2 %all-to-all-done = bf16[16,3072,320]{1,2,0:T(8,128)(2,1)} async-done(((bf16[16,3072,320]{1,2,0:T(8,128)(2,1)}), bf16[16,3072,320]{1,2,0:T(8,128)(2,1)}, u32[]{:S(2)}, u32[]{:S(2)}) %all-to-all-start) | async-done | bytes 31457312 | tf_op jit(solution)/shard_map/all_to_all | solution.py:33
  608.5 17.1 %fusion.5 = f32[256,5120]{0,1:T(8,128)S(1)} fusion(bf16[3072,5120]{0,1:T(8,128)(2,1)} %bitcast.2, bf16[3072,256]{1,0:T(8,128)(2,1)S(1)} %copy-done, f32[1,256,5120]{1,2,0:T(8,128)} %copy.28, f32[]{:T(128)} %convert_reduce_fusion), kind=kOutput, calls=%fused_computation.8 | convolution fusion | flops 8055685120 | bytes 43515908 | tf_op jit(solution)/shard_map/dot_general | solution.py:30
  625.7 3.2 fusion.18
  628.9 15.1 %all_to_all.15 = f32[8,256,64]{1,2,0:T(8,128)S(1)} all-to-all(f32[8,256,64]{1,2,0:T(8,128)S(1)} %broadcast_in_dim.7), channel_id=1, replica_groups=mesh['dp'=8,'tensor'=16] {'dp'}, dimensions={0} | all-to-all | bytes 1048576 | tf_op jit(solution)/shard_map/all_to_all | solution.py:14
  644.3 0.3 reshape.50
  644.7 17.2 %all_to_all.16 = f32[16,1,4096]{2,1,0:T(1,128)S(1)} all-to-all(f32[16,1,4096]{2,1,0:T(1,128)S(1)} %reshape.50), channel_id=1, replica_groups=mesh['dp'=8,'tensor'=16] {'tensor'}, dimensions={0} | all-to-all | bytes 524288 | tf_op jit(solution)/shard_map/all_to_all | solution.py:14
  661.9 0.5 broadcast.68
  662.4 1.3 reduce.6
  664.0 5.8 cholesky.16
  669.9 0.6 compare_reduce_fusion
  670.6 0.7 fusion.10
  671.2 4.9 custom-call.7
  676.4 8.7 %convolution_multiply_fusion.2 = f32[5120,64]{0,1:T(8,128)} fusion(f32[256,5120]{0,1:T(8,128)} %copy-done.2, f32[64,256]{1,0:T(8,128)S(1)} %fusion.6), kind=kOutput, calls=%fused_computation.9 | convolution fusion | flops 1006960640 | bytes 6619136 | tf_op jit(solution)/shard_map/dot_general | solution.py:43
  685.1 146.8 %all-reduce.2.cloned.1.call-done = f32[5120,64]{0,1:T(8,128)} async-done(((f32[5120,64]{0,1:T(8,128)}), f32[5120,64]{0,1:T(8,128)}) %all-reduce.2.cloned.1.call-update) | async-done | bytes 1310736 | tf_op jit(solution)/shard_map/psum | solution.py:44
  831.9 9.7 %fusion.2 = f32[1,256,5120]{1,2,0:T(8,128)} fusion(f32[256,5120]{0,1:T(8,128)} %copy-done.2, f32[64,256]{1,0:T(8,128)S(1)} %fusion.6, f32[5120,64]{0,1:T(8,128)} %all-reduce.2.cloned.1.call-done), kind=kOutput, calls=%fused_computation.4 | convolution fusion | flops 1009254400 | bytes 11862016 | tf_op jit(solution)/shard_map/dot_general | solution.py:47
  841.6 6.0 copy.31
  848.0 1.4 copy-done.5
  849.4 5.8 fusion.3
  (31 shorter events, 1.4 us)
Async XLA Ops:
  7.2 601.4 %copy-start = (bf16[3072,256]{1,0:T(8,128)(2,1)S(1)}, bf16[3072,256]{1,0:T(8,128)(2,1)}, u32[]{:S(2)}) copy-start(bf16[3072,256]{1,0:T(8,128)(2,1)} %param.7) | copy-start | bytes 4718596
  20.4 588.2 %all-to-all-start = ((bf16[16,3072,320]{1,2,0:T(8,128)(2,1)}), bf16[16,3072,320]{1,2,0:T(8,128)(2,1)}, u32[]{:S(2)}, u32[]{:S(2)}) async-start(bf16[16,3072,320]{1,2,0:T(8,128)(2,1)} %stack.2), calls=%async_computation | async-start | bytes 62914560 | tf_op jit(solution)/shard_map/all_to_all | solution.py:33
  28.8 5.9 copy-start.7
  28.8 803.1 %all-reduce.2.cloned.1.call-start = ((), (), s32[]{:S(2)}) async-start(), calls=%async_computation.3 | async-start | bytes 2621440 | tf_op jit(solution)/shard_map/psum | solution.py:44
  608.5 17.1 %copy-start.6 = (f32[5120,64]{0,1:T(8,128)S(1)}, f32[5120,64]{0,1:T(8,128)}, u32[]{:S(2)}) copy-start(f32[5120,64]{0,1:T(8,128)} %param.11) | copy-start | bytes 3932164
  625.7 3.2 copy-start.2
  841.6 6.0 copy-start.3
  847.6 1.7 copy-start.5
  847.8 7.3 copy-start.1
  849.4 5.8 copy-start.4
Sparse Core Ops, SparseCore 0:
  685.2 146.6 all-reduce.1

commit v2 on v0

--- a/solution.py
+++ b/solution.py
@@ -39,7 +39,7 @@
     factor = jnp.linalg.cholesky(gram)
     ortho = jax.scipy.linalg.solve_triangular(factor, left.T, lower=True).T
     term = lax.dot_general(both, ortho, contract, precision=hi) / replicas
-    right = lax.psum(term, ("dp", "tensor"))
+    right = lax.psum(lax.psum(term, "tensor"), "dp")
     squares = jnp.sum(right * right, axis=0)
     new_right = right * lax.rsqrt(squares + EPS)
     lowrank = jnp.dot(ortho, right.T, precision=hi)

time: 450 us -> 454 us (level)
    psum x1 -> x2, waiting for transfers between devices: 147 us -> 149 us  [per_device(): right = lax.psum(lax.psum(term, 'tensor'), 'dp')]
  transfers between devices with their start and end apart: 2 -> 3, of which waited for: 2 -> 3; matrix products, arithmetic and copies ran while one was open for 1% -> 1% of each run, Pallas kernels for 0% -> 0%
where the time goes in v2:
time: 454 us; the launch traced here: 452 us
  waiting for transfers between devices  332 us (73%)
  matrix products  44.9 us (10%)
  blocking collectives  26.5 us (6%)
  other arithmetic  19.5 us (4%)
  local copies, waits for them, and re-layouts  14.7 us (3%)
  between operations  13.9 us (3%)
    all_gather x1, waiting for transfers between devices, per_device(): lax.all_gather(masked, 'tensor', axis=1, tiled=True)  183 us
    psum x2, waiting for transfers between devices, per_device(): right = lax.psum(lax.psum(term, 'tensor'), 'dp')  149 us
    all_to_all x2, blocking collectives, from_everyone(): lax.all_to_all(jnp.broadcast_to(x[None], (devices, *x.shape)), axis, 0, 0...  26.5 us
    dot_general x1, matrix products, per_device(): lax.dot_general(cotangent, lax.all_gather(masked, 'tensor', axis=1, tiled...  17.1 us
    unnamed x20, local copies, waits for them, and re-layouts  14 us
    dot_general x1, matrix products, per_device(): lowrank = jnp.dot(ortho, right.T, precision=hi)  9.7 us
  transfers between devices with their start and end apart: 3, of which 3 were waited for; matrix products, arithmetic and copies ran while one was open for 1% of the time, Pallas kernels for 0%

profile of v2, /device:TPU:1, one launch (start us, length us, event | category | flops | bytes accessed | tf_op | source)
XLA Modules:
  0.0 451.8 jit_solution(1180807725015690461)
XLA Ops:
  7.2 0.8 fusion.15
  8.1 3.0 broadcast_multiply_fusion
  11.1 5.9 %copy.22 = f32[1,256,5120]{1,2,0:T(8,128)} copy(f32[1,256,5120]{2,1,0:T(8,128)} %param.9) | data formatting | bytes 10485760 | tf_op args[3]
  17.0 0.6 convert_reduce_fusion
  17.6 183.0 %all-gather.2.cloned.1.call-done = bf16[3072,5120]{0,1:T(8,128)(2,1)} async-done(((bf16[3072,320]{0,1:T(8,128)(2,1)}), bf16[3072,5120]{0,1:T(8,128)(2,1)}) %all-gather.2.cloned.1.call-update) | async-done | bytes 31457296 | tf_op jit(solution)/shard_map/all_gather | solution.py:32
  200.6 17.1 %fusion.5 = f32[256,5120]{0,1:T(8,128)S(1)} fusion(bf16[3072,5120]{0,1:T(8,128)(2,1)} %all-gather.2.cloned.1.call-done, bf16[3072,256]{1,0:T(8,128)(2,1)S(1)} %copy-done, f32[1,256,5120]{1,2,0:T(8,128)} %copy.22, f32[]{:T(128)} %convert_reduce_fusion), kind=kOutput, calls=%fused_computation.8 | convolution fusion | flops 8055685120 | bytes 43515908 | tf_op jit(solution)/shard_map/dot_general | solution.py:30
  217.7 3.2 fusion.18
  221.0 14.2 %all_to_all.10 = f32[8,256,64]{1,2,0:T(8,128)S(1)} all-to-all(f32[8,256,64]{1,2,0:T(8,128)S(1)} %broadcast_in_dim.7), channel_id=1, replica_groups=mesh['dp'=8,'tensor'=16] {'dp'}, dimensions={0} | all-to-all | bytes 1048576 | tf_op jit(solution)/shard_map/all_to_all | solution.py:14
  235.5 0.3 reshape.40
  235.8 12.2 %all_to_all.11 = f32[16,1,4096]{2,1,0:T(1,128)S(1)} all-to-all(f32[16,1,4096]{2,1,0:T(1,128)S(1)} %reshape.40), channel_id=1, replica_groups=mesh['dp'=8,'tensor'=16] {'tensor'}, dimensions={0} | all-to-all | bytes 524288 | tf_op jit(solution)/shard_map/all_to_all | solution.py:14
  248.1 0.5 broadcast.66
  248.6 1.3 reduce.6
  250.2 5.8 %cholesky.16 = f32[64,64]{1,0:T(8,128)S(1)} custom-call(f32[64,64]{1,0:T(8,128)S(1)} %fusion.12), custom_call_target="Cholesky" | custom-call | tf_op jit(solution)/shard_map/jit(cholesky)/cholesky | solution.py:39
  256.1 0.6 compare_reduce_fusion
  256.7 0.7 fusion.10
  257.4 4.9 %custom-call.7 = f32[1,64,64]{1,2,0:T(8,128)S(1)} custom-call(f32[1,64,64]{2,1,0:T(8,128)S(1)} %fusion.10), custom_call_target="InvertDiagBlocksLowerTriangular" | custom-call | tf_op jit(solution)/shard_map/jit(_solve_triangular)/triangular_solve | solution.py:40
  262.6 8.7 %convolution_multiply_fusion.2 = f32[5120,64]{0,1:T(8,128)} fusion(f32[256,5120]{0,1:T(8,128)} %copy-done.2, f32[64,256]{1,0:T(8,128)S(1)} %fusion.6), kind=kOutput, calls=%fused_computation.9 | convolution fusion | flops 1006960640 | bytes 6619136 | tf_op jit(solution)/shard_map/dot_general | solution.py:41
  271.6 84.4 %all-reduce.3.cloned.1.call-done = f32[5120,64]{0,1:T(8,128)} async-done(((f32[5120,64]{0,1:T(8,128)}), f32[5120,64]{0,1:T(8,128)}) %all-reduce.3.cloned.1.call-update) | async-done | bytes 1310736 | tf_op jit(solution)/shard_map/psum | solution.py:42
  356.0 64.6 %all-reduce.5.cloned.1.call-done = f32[5120,64]{0,1:T(8,128)} async-done(((f32[5120,64]{0,1:T(8,128)}), f32[5120,64]{0,1:T(8,128)}) %all-reduce.5.cloned.1.call-update) | async-done | bytes 1310736 | tf_op jit(solution)/shard_map/psum | solution.py:42
  420.5 1.5 multiply_reduce_fusion
  422.0 9.7 %fusion.2 = f32[1,256,5120]{1,2,0:T(8,128)} fusion(f32[256,5120]{0,1:T(8,128)} %copy-done.2, f32[64,256]{1,0:T(8,128)S(1)} %fusion.6, f32[5120,64]{0,1:T(8,128)} %all-reduce.5.cloned.1.call-done), kind=kOutput, calls=%fused_computation.4 | convolution fusion | flops 1009254400 | bytes 11862016 | tf_op jit(solution)/shard_map/dot_general | solution.py:45
  431.7 6.0 %copy.25 = f32[1,256,5120]{2,1,0:T(8,128)} copy(f32[1,256,5120]{1,2,0:T(8,128)} %fusion.2) | data formatting | bytes 10485760
  437.9 1.6 copy-done.5
  439.5 5.8 %fusion.3 = bf16[256,5120]{1,0:T(8,128)(2,1)} fusion(f32[64,256]{1,0:T(8,128)S(1)} %fusion.6, f32[5120,64]{0,1:T(8,128)S(1)} %broadcast_multiply_fusion.1, bf16[256,5120]{1,0:T(8,128)(2,1)S(1)} %copy-done.5), kind=kOutput, calls=%fused_computation.5 | convolution fusion | flops 1011875840 | bytes 6619136 | tf_op jit(solution)/shard_map/dot_general | solution.py:48
  (34 shorter events, 1.6 us)
Async XLA Ops:
  7.2 193.5 %copy-start = (bf16[3072,256]{1,0:T(8,128)(2,1)S(1)}, bf16[3072,256]{1,0:T(8,128)(2,1)}, u32[]{:S(2)}) copy-start(bf16[3072,256]{1,0:T(8,128)(2,1)} %param.7) | copy-start | bytes 4718596
  7.2 193.5 %all-gather.2.cloned.1.call-start = ((), (), s32[]{:S(2)}) async-start(), calls=%async_computation.2 | async-start | bytes 33423360 | tf_op jit(solution)/shard_map/all_gather | solution.py:32
  11.1 5.9 %copy-start.7 = (s32[8]{0:T(128)S(1)}, s32[8]{0:T(128)}, u32[]{:S(2)}) copy-start(s32[8]{0:T(128)} %param.8) | copy-start | bytes 100
  11.1 344.9 %all-reduce.3.cloned.1.call-start = ((), (), s32[]{:S(2)}) async-start(), calls=%async_computation.3 | async-start | bytes 2621440 | tf_op jit(solution)/shard_map/psum | solution.py:42
  17.6 200.1 %copy-start.6 = (f32[5120,64]{0,1:T(8,128)S(1)}, f32[5120,64]{0,1:T(8,128)}, u32[]{:S(2)}) copy-start(f32[5120,64]{0,1:T(8,128)} %param.11) | copy-start | bytes 3932164
  217.7 3.2 copy-start.2
  271.3 149.2 %all-reduce.5.cloned.1.call-start = ((), (), s32[]{:S(2)}) async-start(), calls=%async_computation.4 | async-start | bytes 2621440 | tf_op jit(solution)/shard_map/psum | solution.py:42
  431.7 6.0 %copy-start.3 = (f32[5120,64]{0,1:T(8,128)S(1)}, f32[5120,64]{0,1:T(8,128)}, u32[]{:S(2)}) copy-start(f32[5120,64]{0,1:T(8,128)} %all-reduce.5.cloned.1.call-done) | copy-start | bytes 3932164
  437.7 1.7 copy-start.5
  437.7 7.6 %copy-start.1 = (bf16[3072,256]{1,0:T(8,128)(2,1)S(1)}, bf16[3072,256]{1,0:T(8,128)(2,1)}, u32[]{:S(2)}) copy-start(bf16[3072,256]{1,0:T(8,128)(2,1)} %param.7) | copy-start | bytes 4718596
  439.5 5.8 %copy-start.4 = (f32[5120,64]{0,1:T(8,128)}, f32[5120,64]{0,1:T(8,128)S(1)}, u32[]{:S(2)}) copy-start(f32[5120,64]{0,1:T(8,128)S(1)} %broadcast_multiply_fusion.1) | copy-start | bytes 3932164
Sparse Core Ops, SparseCore 0:
  11.2 189.4 all-gather.1
  271.4 84.4 all-reduce.2
  358.3 62.1 all-reduce.4
